TPU v7x, 32 devices: a whole 2x2x4 slice. The times are simulated.
32 devices in a mesh: row: 4 (over y, core), col: 8 (over z, x).
Axes of the slice: x: 2, y: 2, z: 4, core: 2. Of those that a mesh axis runs over, the one named last changes fastest.
Arguments:
- l_saved: bfloat16 [16, 4, 256, 8, 256], P(None, 'row', None, 'col'), as said below
- l_grad: bfloat16 [16, 4, 256, 8, 256], P(None, 'row', None, 'col'), as said below
Outputs:
- grad_out: float32 [16, 4, 256, 8, 256], P(None, 'row', None, 'col')
Inputs may be any that keep to these rules, and one draw needn't show every extreme that they name: Read as one matrix of 16384 rows, l_saved is lower triangular with its diagonal between 1 and 2. Read as one matrix, l_grad is zero above the diagonal.
All inputs are finite; a program needn't handle non-finite values.
Results may differ from a plain program's by a relative error of at most 0.0003.
Values may be sent and summed in bfloat16 or wider, within the bound.
A program may use at most 64 MiB of HBM per device.

v0:
```python
import jax
import jax.numpy as jnp
from jax import lax
from jax.sharding import PartitionSpec as P

F32 = jnp.float32
BF16 = jnp.bfloat16
HIGH3 = lax.Precision.HIGH


def dot3(a, b, ca=1, cb=0):
    return lax.dot_general(
        a, b, (((ca,), (cb,)), ((), ())), precision=HIGH3, preferred_element_type=F32
    )


def bdot(a, b):
    return lax.dot_general(
        a, b, (((2,), (1,)), ((0,), (0,))), precision=HIGH3, preferred_element_type=F32
    )


def inverse_pair(tiles):
    tile = tiles.shape[-1]
    rows = lax.broadcasted_iota(jnp.int32, (tile, tile), 0)
    cols = lax.broadcasted_iota(jnp.int32, (tile, tile), 1)
    eye = (rows == cols).astype(F32)
    recip = 1.0 / jnp.sum(tiles * eye, axis=2)
    inv = eye * recip[:, None, :]
    size = 1
    while size < tile:
        off = (rows // size % 2 == 1) & (cols // size == rows // size - 1)
        part = jnp.where(off, tiles, 0.0)
        if size == 1:
            inv = inv - recip[:, :, None] * part * recip[:, None, :]
        else:
            inv = inv - bdot(inv, bdot(part, inv))
        size *= 2
    return inv


def per_device(l_saved, l_grad):
    rows_here, tile = (l_saved.shape[0], l_saved.shape[2])
    n_row = lax.axis_size("row")
    n_col = lax.axis_size("col")
    factor = l_saved.reshape(rows_here, tile, tile)
    grad = l_grad.reshape(rows_here, tile, tile)
    my_row = lax.axis_index("row")
    my_col = lax.axis_index("col")
    assert n_col % n_row == 0
    first = n_col // n_row
    loc = first - 1
    lo, hi = (n_col - 2, n_col - 1)
    l_dk = lax.all_gather(factor[loc], "row")[n_row - 2 :].reshape(2 * tile, tile)
    mine = jnp.concatenate([l_dk, grad[first:].reshape(-1, tile)], 0)
    zero = jnp.zeros_like(mine)
    both = jnp.concatenate(
        [jnp.where(my_col == lo, mine, zero), jnp.where(my_col == hi, mine, zero)], 1
    )
    both = lax.psum(both, "col")
    l_dd = both[: 2 * tile].astype(F32)
    g_d = both[2 * tile :]
    l66, l76, l77 = (l_dd[:tile, :tile], l_dd[tile:, :tile], l_dd[tile:, tile:])
    inv = inverse_pair(jnp.stack([l66, l77]))
    w76 = -dot3(inv[1], dot3(l76, inv[0]))
    w = jnp.concatenate(
        [jnp.concatenate([inv[0], jnp.zeros_like(w76)], 1), jnp.concatenate([w76, inv[1]], 1)], 0
    )
    below_l = factor[first:].reshape(-1, tile)
    h = lax.dot_general(g_d, below_l, (((0,), (0,)), ((), ())), preferred_element_type=F32)
    t = dot3(w, lax.psum(h, "row"), 0, 0)
    fresh = grad[loc].astype(F32)
    g_dk = lax.all_gather(grad[loc], "row")[n_row - 2 :].reshape(2 * tile, tile).astype(F32)
    q_mine = g_dk - t
    z2 = jnp.zeros_like(q_mine)
    q = lax.psum(
        jnp.concatenate(
            [jnp.where(my_col == lo, q_mine, z2), jnp.where(my_col == hi, q_mine, z2)], 1
        ),
        "col",
    )
    eye2 = jnp.eye(2 * tile, dtype=F32)
    q = jnp.tril(q)
    m = dot3(l_dd, q, 0, 0)
    phi = jnp.tril(m) - 0.5 * m * eye2
    half = dot3(dot3(w, phi, 0, 0), w)
    s = half + half.T
    out_dd = jnp.tril(s) - 0.5 * s * eye2
    right = my_col >= lo
    w_mine = jnp.where(my_col == lo, w[:, :tile], w[:, tile:])
    x = jnp.where(right, -w_mine, dot3(w, l_dk.astype(F32)))
    x_hi = lax.reduce_precision(x, 8, 7)
    x_lo = (x - x_hi).astype(BF16)
    x_hi = x_hi.astype(BF16)
    prod = jnp.dot(g_d, x_hi, preferred_element_type=F32) + jnp.dot(
        g_d, x_lo, preferred_element_type=F32
    )
    base = jnp.where(right, jnp.zeros((), BF16), grad[first:]).astype(F32)
    low = base - prod.reshape(-1, tile, tile)
    at_lo = my_row == n_row - 2
    s_row = jnp.where(at_lo, s[:tile], s[tile:])
    t_row = jnp.where(at_lo, t[:tile], t[tile:])
    own = fresh - (t_row + dot3(s_row, l_dk.astype(F32)))
    d_row = jnp.where(at_lo, out_dd[:tile], out_dd[tile:])
    d_own = jnp.where(my_col == lo, d_row[:, :tile], d_row[:, tile:])
    in_panel = my_row >= n_row - 2
    zt = jnp.zeros_like(fresh)
    own = jnp.where(in_panel, jnp.where(right, d_own, own), jnp.where(right, zt, fresh))
    upper = jnp.where(right, jnp.zeros((), BF16), grad[:loc]).astype(F32)
    out = jnp.concatenate([upper, own[None], low], 0)
    return out.reshape(l_grad.shape)


def solution(mesh):
    spec = P(None, "row", None, "col", None)
    return jax.shard_map(
        per_device, mesh=mesh, in_specs=(spec, spec), out_specs=spec, check_vma=False
    )
```

profile of v0, /device:TPU:0, one launch (start us, length us, event | category | flops | bytes accessed | tf_op | source)
XLA Modules:
  0.0 323.6 jit_solution(8879946724786427271)
XLA Ops:
  6.5 0.9 slice.87
  7.5 8.7 %all-gather = bf16[4,1,256,1,256]{4,2,3,1,0:T(8,128)(2,1)S(1)} all-gather(bf16[1,1,256,1,256]{4,2,3,1,0:T(8,128)(2,1)S(1)} %slice.87), channel_id=2, replica_groups=mesh['row'=4,'col'=8] {'row'}, dimensions={0}, use_global_device_ids=true | all-gather | bytes 655360 | tf_op jit(solution)/shard_map/all_gather | solution.py:54
  16.2 0.0 copy-start.6
  16.2 1.7 slice.115
  17.9 0.7 broadcast_select_fusion.1
  18.6 2.3 pad_maximum_fusion
  20.9 0.0 all-reduce.5.cloned.1.call-update
  20.9 0.0 all-reduce.7.cloned.1.call-start
  21.0 1.5 copy-done.3
  22.5 0.7 bitcast_convert_fusion
  23.2 7.3 %all-gather.1 = bf16[4,1,256,1,256]{4,2,3,1,0:T(8,128)(2,1)S(1)} all-gather(bf16[1,1,256,1,256]{4,2,3,1,0:T(8,128)(2,1)S(1)} %get-tuple-element.8), channel_id=3, replica_groups=mesh['row'=4,'col'=8] {'row'}, dimensions={0}, use_global_device_ids=true | all-gather | bytes 655360 | tf_op jit(solution)/shard_map/all_gather | solution.py:73
  30.5 0.7 slice.122
  31.5 0.2 fusion.85
  31.7 0.2 fusion.84
  31.9 0.2 fusion.83
  32.1 0.2 fusion.82
  32.3 0.2 fusion.81
  32.5 0.2 fusion.80
  32.7 0.2 fusion.79
  32.9 145.4 %all-reduce.5.cloned.1.call-done = bf16[4096,512]{1,0:T(8,128)(2,1)} async-done(((bf16[4096,512]{1,0:T(8,128)(2,1)}), bf16[4096,512]{1,0:T(8,128)(2,1)}) %all-reduce.5.cloned.1.call-update) | async-done | bytes 4194320 | tf_op jit(solution)/shard_map/psum | solution.py:60
  178.3 1.2 slice_convert_fusion
  179.5 0.1 multiply_reduce_fusion
  179.7 0.5 fusion.34
  180.2 0.5 convolution_subtract_fusion.6
  180.7 0.4 fusion.32
  181.1 0.4 convolution_subtract_fusion.5
  181.5 0.4 fusion.30
  181.9 0.4 convolution_subtract_fusion.4
  182.3 0.4 fusion.28
  182.7 0.4 convolution_subtract_fusion.3
  183.1 0.4 fusion.26
  183.5 0.4 convolution_subtract_fusion.2
  183.9 0.4 fusion.24
  184.3 0.0 slice-start
  184.3 0.4 convolution_subtract_fusion.1
  184.7 0.4 fusion.22
  185.2 0.4 convolution_subtract_fusion
  185.6 0.5 copy-done
  186.1 0.2 fusion.99
  186.4 0.3 convolution_negate_fusion
  186.6 0.2 slice-done
  186.8 1.9 fusion.3
  188.7 0.0 all-reduce.7.cloned.1.call-update
  188.8 0.2 all-reduce.9.cloned.1.call-start
  189.0 0.1 select_maximum_fusion
  189.1 1.4 convolution_select_fusion
  190.5 30.8 %all-reduce.7.cloned.1.call-done = f32[512,256]{1,0:T(8,128)} async-done(((f32[512,256]{1,0:T(8,128)}), f32[512,256]{1,0:T(8,128)}) %all-reduce.7.cloned.1.call-update) | async-done | bytes 524304 | tf_op jit(solution)/shard_map/psum | solution.py:71
  221.3 2.7 fusion.40
  224.0 1.2 pad_maximum_fusion.3
  225.2 0.0 all-reduce.9.cloned.1.call-update
  225.2 3.3 %fusion.1 = f32[3584,256]{1,0:T(8,128)S(1)} fusion(bf16[4096,512]{1,0:T(8,128)(2,1)} %all-reduce.5.cloned.1.call-done, f32[512,256]{1,0:T(8,128)S(1)} %convolution_select_fusion), kind=kOutput, calls=%fused_computation.5 | convolution fusion | flops 939786240 | bytes 7864320 | tf_op jit(solution)/shard_map/dot_general | solution.py:95
  228.5 1.1 convolution_add_fusion
  229.7 2.3 convert_subtract_fusion
  231.9 71.8 %all-reduce.9.cloned.1.call-done = f32[512,512]{1,0:T(8,128)} async-done(((f32[512,512]{1,0:T(8,128)}), f32[512,512]{1,0:T(8,128)}) %all-reduce.9.cloned.1.call-update) | async-done | bytes 1048592 | tf_op jit(solution)/shard_map/psum | solution.py:76
  303.7 2.2 fusion.14
  305.9 1.0 fusion.9
  307.0 2.0 fusion.113
  309.0 1.3 copy.12
  310.3 1.6 select_subtract_fusion
  311.9 0.1 slice_select_fusion.3
  312.1 0.3 fusion.8
  312.4 0.5 copy-done.2
  312.8 0.4 pad_maximum_fusion.1
  313.2 3.9 %reshape.79 = f32[16,1,256,1,256]{4,3,2,1,0:T(1,128)} reshape(f32[16,256,256]{2,1,0:T(8,128)S(1)} %pad_maximum_fusion.1) | data formatting | bytes 8388608 | tf_op jit(solution)/shard_map/reshape | solution.py:111
  (37 shorter events, 0.3 us)
Async XLA Ops:
  6.5 171.8 %all-reduce.5.cloned.1.call-start = ((), (), s32[]{:S(2)}) async-start(), calls=%async_computation | async-start | bytes 8388608 | tf_op jit(solution)/shard_map/psum | solution.py:60
  16.2 2.4 copy-start.6
  20.9 1.6 copy-start.3
  20.9 200.4 %all-reduce.7.cloned.1.call-start = ((), (), s32[]{:S(2)}) async-start(), calls=%async_computation.1 | async-start | bytes 1048576 | tf_op jit(solution)/shard_map/psum | solution.py:71
  183.9 2.2 copy-start
  184.3 2.5 slice-start
  186.1 119.8 %copy-start.4 = (f32[256,256]{1,0:T(8,128)}, f32[256,256]{1,0:T(8,128)S(1)}, u32[]{:S(2)}) copy-start(f32[256,256]{1,0:T(8,128)S(1)} %get-tuple-element.15) | copy-start | bytes 786436
  186.1 119.8 %copy-start.5 = (f32[256,256]{1,0:T(8,128)}, f32[256,256]{1,0:T(8,128)S(1)}, u32[]{:S(2)}) copy-start(f32[256,256]{1,0:T(8,128)S(1)} %get-tuple-element.16) | copy-start | bytes 786436
  188.8 115.0 %all-reduce.9.cloned.1.call-start = ((), (), s32[]{:S(2)}) async-start(), calls=%async_computation.2 | async-start | bytes 2097152 | tf_op jit(solution)/shard_map/psum | solution.py:76
  225.2 3.3 %copy-start.1 = (bf16[4096,512]{1,0:T(8,128)(2,1)S(1)}, bf16[4096,512]{1,0:T(8,128)(2,1)}, u32[]{:S(2)}) copy-start(bf16[4096,512]{1,0:T(8,128)(2,1)} %all-reduce.5.cloned.1.call-done) | copy-start | bytes 12582916
  309.0 3.1 copy-start.7
  310.3 1.7 copy-start.9
  310.3 2.5 copy-start.2
  310.3 2.5 copy-start.8
Sparse Core Ops, SparseCore 0:
  21.1 157.1 all-reduce.4
  188.9 32.3 all-reduce.6
  225.3 78.3 all-reduce.8
where the time goes:
time: 324 us
  waiting for transfers between devices  248 us (77%)
  matrix products  22.3 us (7%)
  blocking collectives  15.9 us (5%)
  between operations  13.6 us (4%)
  other arithmetic  12.1 us (4%)
  local copies, waits for them, and re-layouts  11.3 us (3%)
    psum x1, waiting for transfers between devices, per_device(): both = lax.psum(both, 'col')  145 us
    psum x1, waiting for transfers between devices, per_device(): lax.psum(jnp.concatenate([jnp.where(my_col == lo, q_mine, z2), jnp.where(...  71.8 us
    psum x1, waiting for transfers between devices, per_device(): t = dot3(w, lax.psum(h, 'row'), 0, 0)  30.8 us
    dot_general x8, matrix products, dot3(): lax.dot_general(a, b, (((ca,), (cb,)), ((), ())), precision=HIGH3, prefer...  10.1 us
    all_gather x1, blocking collectives, per_device(): lax.all_gather(factor[loc], 'row')[n_row - 2:].reshape(2 * tile, tile)  8.68 us
    all_gather x1, blocking collectives, per_device(): lax.all_gather(grad[loc], 'row')[n_row - 2:].reshape(2 * tile, tile)  7.26 us
  transfers between devices with their start and end apart: 3, of which 3 were waited for; matrix products, arithmetic and copies ran while one was open for 3% of the time, Pallas kernels for 0%

commit v1 on v0

--- a/solution.py
+++ b/solution.py
@@ -57,7 +57,11 @@
     both = jnp.concatenate(
         [jnp.where(my_col == lo, mine, zero), jnp.where(my_col == hi, mine, zero)], 1
     )
-    both = lax.psum(both, "col")
+    count, total = (lax.axis_size("col"), both)
+    for far in [1 << k for k in range(count.bit_length() - 1)]:
+        swap = [(i, i ^ far) for i in range(count)]
+        total = total + lax.ppermute(total, "col", swap)
+    both = total
     l_dd = both[: 2 * tile].astype(F32)
     g_d = both[2 * tile :]
     l66, l76, l77 = (l_dd[:tile, :tile], l_dd[tile:, :tile], l_dd[tile:, tile:])

time: 324 us -> 541 us (1.67)
  waiting for transfers between devices: 248 us -> 456 us
  other arithmetic: 12.1 us -> 18.2 us
  starting transfers between devices: 0.27 us -> 6.05 us
    ppermute x0 -> x3, waiting for transfers between devices: none -> 351 us  [per_device(): total = total + lax.ppermute(total, 'col', swap)]
    psum x1 -> x0, waiting for transfers between devices: 145 us -> none  [per_device(): both = lax.psum(both, 'col')]
    add x0 -> x3, other arithmetic: none -> 9.18 us  [per_device(): total = total + lax.ppermute(total, 'col', swap)]
    ppermute x0 -> x3, starting transfers between devices: none -> 5.79 us  [per_device(): total = total + lax.ppermute(total, 'col', swap)]
  transfers between devices with their start and end apart: 3 -> 5, of which waited for: 3 -> 5; matrix products, arithmetic and copies ran while one was open for 3% -> 2% of each run, Pallas kernels for 0% -> 0%
where the time goes in v1:
time: 541 us
  waiting for transfers between devices  456 us (84%)
  matrix products  22.3 us (4%)
  other arithmetic  18.2 us (3%)
  blocking collectives  15.6 us (3%)
  between operations  13.9 us (3%)
  local copies, waits for them, and re-layouts  9.13 us (2%)
  starting transfers between devices  6.05 us (1%)
    ppermute x3, waiting for transfers between devices, per_device(): total = total + lax.ppermute(total, 'col', swap)  351 us
    psum x1, waiting for transfers between devices, per_device(): lax.psum(jnp.concatenate([jnp.where(my_col == lo, q_mine, z2), jnp.where(...  71.8 us
    psum x1, waiting for transfers between devices, per_device(): t = dot3(w, lax.psum(h, 'row'), 0, 0)  32.4 us
  transfers between devices with their start and end apart: 5, of which 5 were waited for; matrix products, arithmetic and copies ran while one was open for 2% of the time, Pallas kernels for 0%

profile of v1, /device:TPU:0, one launch (start us, length us, event | category | flops | bytes accessed | tf_op | source)
XLA Modules:
  0.0 540.9 jit_solution(16961997449021672686)
XLA Ops:
  6.5 0.9 slice.87
  7.5 8.7 %all-gather = bf16[4,1,256,1,256]{4,2,3,1,0:T(8,128)(2,1)S(1)} all-gather(bf16[1,1,256,1,256]{4,2,3,1,0:T(8,128)(2,1)S(1)} %slice.87), channel_id=2, replica_groups=mesh['row'=4,'col'=8] {'row'}, dimensions={0}, use_global_device_ids=true | all-gather | bytes 655360 | tf_op jit(solution)/shard_map/all_gather | solution.py:54
  16.2 1.7 slice.115
  17.9 0.7 broadcast_select_fusion.1
  18.6 0.3 pad_maximum_fusion
  18.9 1.6 collective-permute-start
  20.5 91.3 %collective-permute-done = bf16[4096,512]{1,0:T(8,128)(2,1)S(1)} collective-permute-done((bf16[4096,512]{1,0:T(8,128)(2,1)S(1)}, bf16[4096,512]{1,0:T(8,128)(2,1)S(1)}, u32[]{:S(2)}, u32[]{:S(2)}) %collective-permute-start) | collective-permute-done | bytes 4194336 | tf_op jit(solution)/shard_map/ppermute | solution.py:63
  111.8 1.1 fusion.115
  112.9 1.6 collective-permute-start.1
  114.6 90.4 %collective-permute-done.1 = bf16[4096,512]{1,0:T(8,128)(2,1)S(1)} collective-permute-done((bf16[4096,512]{1,0:T(8,128)(2,1)S(1)}, bf16[4096,512]{1,0:T(8,128)(2,1)S(1)}, u32[]{:S(2)}, u32[]{:S(2)}) %collective-permute-start.1) | collective-permute-done | bytes 4194336 | tf_op jit(solution)/shard_map/ppermute | solution.py:63
  205.0 3.4 add.99
  208.4 2.6 collective-permute-start.2
  211.0 0.7 bitcast_convert_fusion
  211.7 6.9 %all-gather.1 = bf16[4,1,256,1,256]{4,2,3,1,0:T(8,128)(2,1)S(1)} all-gather(bf16[1,1,256,1,256]{4,2,3,1,0:T(8,128)(2,1)S(1)} %get-tuple-element.8), channel_id=3, replica_groups=mesh['row'=4,'col'=8] {'row'}, dimensions={0}, use_global_device_ids=true | all-gather | bytes 655360 | tf_op jit(solution)/shard_map/all_gather | solution.py:77
  218.6 0.7 slice.122
  219.5 0.1 fusion.86
  219.6 0.2 fusion.85
  219.8 0.2 fusion.84
  220.0 0.2 fusion.83
  220.2 0.2 fusion.82
  220.4 0.2 fusion.81
  220.6 0.2 fusion.80
  220.8 0.2 fusion.79
  221.0 169.6 %collective-permute-done.2 = bf16[4096,512]{1,0:T(8,128)(2,1)} collective-permute-done((bf16[4096,512]{1,0:T(8,128)(2,1)}, bf16[4096,512]{1,0:T(8,128)(2,1)}, u32[]{:S(2)}, u32[]{:S(2)}) %collective-permute-start.2) | collective-permute-done | bytes 4194336 | tf_op jit(solution)/shard_map/ppermute | solution.py:63
  390.6 4.7 add.100
  395.3 0.1 slice_convert_fusion
  395.4 0.2 multiply_reduce_fusion
  395.6 0.5 fusion.34
  396.2 0.5 convolution_subtract_fusion.6
  396.7 0.4 fusion.32
  397.1 0.4 convolution_subtract_fusion.5
  397.5 0.4 fusion.30
  397.9 0.4 convolution_subtract_fusion.4
  398.3 0.4 fusion.28
  398.7 0.4 convolution_subtract_fusion.3
  399.1 0.4 fusion.26
  399.5 0.4 convolution_subtract_fusion.2
  399.9 0.4 fusion.24
  400.3 0.4 convolution_subtract_fusion.1
  400.7 0.4 fusion.22
  401.1 0.4 convolution_subtract_fusion
  401.5 0.2 fusion.99
  401.8 0.3 convolution_negate_fusion
  402.1 2.0 fusion.3
  404.1 0.3 all-reduce.6.cloned.1.call-start
  404.4 0.1 select_maximum_fusion
  404.5 1.4 convolution_select_fusion
  405.9 32.4 %all-reduce.4.cloned.1.call-done = f32[512,256]{1,0:T(8,128)} async-done(((f32[512,256]{1,0:T(8,128)}), f32[512,256]{1,0:T(8,128)}) %all-reduce.4.cloned.1.call-update) | async-done | bytes 524304 | tf_op jit(solution)/shard_map/psum | solution.py:75
  438.3 2.7 fusion.40
  441.1 1.1 pad_maximum_fusion.3
  442.2 3.3 fusion
  445.6 1.1 convolution_add_fusion
  446.7 2.2 convert_subtract_fusion
  448.9 71.8 %all-reduce.6.cloned.1.call-done = f32[512,512]{1,0:T(8,128)} async-done(((f32[512,512]{1,0:T(8,128)}), f32[512,512]{1,0:T(8,128)}) %all-reduce.6.cloned.1.call-update) | async-done | bytes 1048592 | tf_op jit(solution)/shard_map/psum | solution.py:80
  520.7 2.2 fusion.14
  522.9 1.0 fusion.9
  523.9 2.0 fusion.113
  525.9 1.3 copy.12
  527.2 1.6 select_subtract_fusion
  528.9 0.1 slice_select_fusion.3
  529.0 0.3 fusion.8
  529.3 0.4 copy-done.2
  529.8 0.4 pad_maximum_fusion.1
  530.2 3.9 reshape.79
  (42 shorter events, 0.3 us)
Async XLA Ops:
  6.5 431.8 %all-reduce.4.cloned.1.call-start = ((), (), s32[]{:S(2)}) async-start(), calls=%async_computation | async-start | bytes 1048576 | tf_op jit(solution)/shard_map/psum | solution.py:75
  16.2 2.4 copy-start.6
  18.9 92.9 %collective-permute-start = (bf16[4096,512]{1,0:T(8,128)(2,1)S(1)}, bf16[4096,512]{1,0:T(8,128)(2,1)S(1)}, u32[]{:S(2)}, u32[]{:S(2)}) collective-permute-start(bf16[4096,512]{1,0:T(8,128)(2,1)S(1)} %pad_maximum_fusion), channel_id=1, source_target_pairs={{0,1},{1,0},{2,3},{3,2},{4,5},{5,4},{6,7},{7,6},{8,9},{9,8},{10,11... | collective-permute-start | bytes 12582920 | tf_op jit(solution)/shard_map/ppermute | solution.py:63
  112.9 98.0 %copy-start.3 = (bf16[16,1,256,1,256]{4,2,3,1,0:T(8,128)(2,1)S(1)}, bf16[16,1,256,1,256]{4,2,3,1,0:T(8,128)(2,1)}, u32[]{:S(2)}) copy-start(bf16[16,1,256,1,256]{4,2,3,1,0:T(8,128)(2,1)} %param.3) | copy-start | bytes 6291460
  112.9 92.0 %collective-permute-start.1 = (bf16[4096,512]{1,0:T(8,128)(2,1)S(1)}, bf16[4096,512]{1,0:T(8,128)(2,1)S(1)}, u32[]{:S(2)}, u32[]{:S(2)}) collective-permute-start(bf16[4096,512]{1,0:T(8,128)(2,1)S(1)} %fusion.115), channel_id=1, source_target_pairs={{0,2},{1,3},{2,0},{3,1},{4,6},{5,7},{6,4},{7,5},{8,10},{9,11},{10,... | collective-permute-start | bytes 12582920 | tf_op jit(solution)/shard_map/ppermute | solution.py:63
  208.4 182.2 %collective-permute-start.2 = (bf16[4096,512]{1,0:T(8,128)(2,1)}, bf16[4096,512]{1,0:T(8,128)(2,1)}, u32[]{:S(2)}, u32[]{:S(2)}) collective-permute-start(bf16[4096,512]{1,0:T(8,128)(2,1)} %add.99), channel_id=1, source_target_pairs={{0,4},{1,5},{2,6},{3,7},{4,0},{5,1},{6,2},{7,3},{8,12},{9,13},{10,... | collective-permute-start | bytes 12582920 | tf_op jit(solution)/shard_map/ppermute | solution.py:63
  395.2 6.9 %copy-start = (bf16[4096,512]{1,0:T(8,128)(2,1)}, bf16[4096,512]{1,0:T(8,128)(2,1)S(1)}, u32[]{:S(2)}) copy-start(bf16[4096,512]{1,0:T(8,128)(2,1)S(1)} %add.100) | copy-start | bytes 12582916
  399.9 2.2 slice-start
  401.8 121.0 %copy-start.4 = (f32[256,256]{1,0:T(8,128)}, f32[256,256]{1,0:T(8,128)S(1)}, u32[]{:S(2)}) copy-start(f32[256,256]{1,0:T(8,128)S(1)} %get-tuple-element.15) | copy-start | bytes 786436
  401.8 121.0 %copy-start.5 = (f32[256,256]{1,0:T(8,128)}, f32[256,256]{1,0:T(8,128)S(1)}, u32[]{:S(2)}) copy-start(f32[256,256]{1,0:T(8,128)S(1)} %get-tuple-element.16) | copy-start | bytes 786436
  404.1 116.6 %all-reduce.6.cloned.1.call-start = ((), (), s32[]{:S(2)}) async-start(), calls=%async_computation.1 | async-start | bytes 2097152 | tf_op jit(solution)/shard_map/psum | solution.py:80
  442.2 3.3 copy-start.1
  525.9 3.0 copy-start.7
  527.2 1.7 copy-start.9
  527.2 2.5 copy-start.2
  527.2 2.5 copy-start.8
Sparse Core Ops, SparseCore 0:
  404.2 34.0 all-reduce.3
  442.4 78.2 all-reduce.5
